TPU v7x, 256 devices: a whole 4x4x8 slice. The times are simulated.
256 devices in a mesh: expert: 8 (over x, core), replica: 32 (over y, z).
Axes of the slice: x: 4, y: 4, z: 8, core: 2. Of those that a mesh axis runs over, the one named last changes fastest.
Arguments:
- tokens: bfloat16 [1536, 4096], P(('expert', 'replica')), may hold values from -6 to 6
- out_grad: bfloat16 [1536, 4096], P(('expert', 'replica')), may hold values from -2.5 to 2.5
- expert_ids: int32 [1536, 2], P(('expert', 'replica')), may hold values from 0 to 7, all different within a row; in each aligned block of 6 rows (0 to 5, 6 to 11, ...) at most 2 rows name the same one
- gates: float32 [1536, 2], P(('expert', 'replica')), may hold values from 0.1 to 1
- w_gate: bfloat16 [8, 7168, 4096], P('expert', 'replica'), may hold values from -0.09375 to 0.09375
- w_up: bfloat16 [8, 7168, 4096], P('expert', 'replica'), may hold values from -0.09375 to 0.09375
- w_down: bfloat16 [8, 7168, 4096], P('expert', 'replica'), may hold values from -0.0625 to 0.0625
Outputs:
- gate_grad: float32 [1536, 2], P(('expert', 'replica'))
- input_grad: bfloat16 [1536, 4096], P(('expert', 'replica'))
- grad_gate: bfloat16 [8, 7168, 4096], P('expert', 'replica')
- grad_up: bfloat16 [8, 7168, 4096], P('expert', 'replica')
- grad_down: bfloat16 [8, 7168, 4096], P('expert', 'replica')
Inputs may be any that keep to these rules, and one draw needn't show every extreme that they name: `expert_ids`: each row names 2 different experts; among the rows of one device no expert is named more than 2 times.
All inputs are finite; a program needn't handle non-finite values.
Results may differ from a plain program's by a relative error of at most 0.02.
Values may be sent and summed in bfloat16 or wider, within the bound.
No kernel may reach another device: no remote copies, remote signals or barrier semaphores. Data moves between devices by JAX's collectives and lax.ppermute only.
A program may use at most 128 MiB of HBM per device.

v0:
```python
import jax
import jax.numpy as jnp
from jax import lax
from jax.sharding import Mesh
from jax.sharding import PartitionSpec as P

REPLICA = ("replica_0", "replica_1")
EXPERT_REPLICA = ("expert", "replica_0", "replica_1")


def split_up(value, dim, peers):
    shape = value.shape
    tiles = value.reshape(*shape[:dim], peers, shape[dim] // peers, *shape[dim + 1 :])
    return jnp.moveaxis(tiles, dim, 0)


def sum_at_owner(value, axis, dim):
    peers = lax.axis_size(axis)
    tiles = lax.all_to_all(split_up(value, dim, peers), axis, 0, 0, tiled=True)
    return jnp.sum(tiles, axis=0)


def own_rows(terms, axes):
    running = terms.astype(jnp.bfloat16)
    for axis in axes:
        running = lax.psum_scatter(running, axis, scatter_dimension=0, tiled=True)
    return running.astype(jnp.float32)


def on_device(tokens, out_grad, expert_ids, gates, w_gate, w_up, w_down):
    token_count = tokens.shape[0]
    fan_out = expert_ids.shape[1]
    model_width = tokens.shape[1]
    owners = lax.axis_size("expert")
    capacity = max(2, 4 * token_count * fan_out // (3 * owners))
    slot_count = owners * capacity
    flat_ids = expert_ids.reshape(-1)
    sequence_pos = jnp.arange(token_count * fan_out, dtype=jnp.int32)
    earlier = sequence_pos[None, :] < sequence_pos[:, None]
    same_expert = flat_ids[:, None] == flat_ids[None, :]
    slot_rank = jnp.sum(jnp.logical_and(same_expert, earlier), axis=1)
    target = flat_ids * capacity + slot_rank
    token_hot = (target[:, None] == jnp.arange(slot_count, dtype=jnp.int32)[None, :]).astype(
        jnp.float32
    )
    token_hot = token_hot.reshape(token_count, fan_out, slot_count)
    dispatch = jnp.sum(token_hot, axis=1).astype(jnp.bfloat16)
    slot_gate = jnp.sum(token_hot * gates[:, :, None], axis=(0, 1)).reshape(owners, capacity)
    leading = (((0,), (0,)), ((), ()))
    contract = (((1,), (1,)), ((), ()))
    send_inputs = (
        lax.dot_general(dispatch, tokens, leading, preferred_element_type=jnp.float32)
        .astype(jnp.bfloat16)
        .reshape(owners, capacity, model_width)
    )
    send_grads = (
        lax.dot_general(dispatch, out_grad, leading, preferred_element_type=jnp.float32)
        .astype(jnp.bfloat16)
        .reshape(owners, capacity, model_width)
    )
    gate_weight = w_gate[0]
    up_weight = w_up[0]
    down_weight = w_down[0]
    owned = (
        lax.all_to_all(send_inputs, "expert", split_axis=0, concat_axis=0, tiled=True),
        lax.all_to_all(send_grads, "expert", split_axis=0, concat_axis=0, tiled=True),
        lax.all_to_all(
            slot_gate.astype(jnp.bfloat16), "expert", split_axis=0, concat_axis=0, tiled=True
        ).astype(slot_gate.dtype),
    )
    column_inputs, column_grads, column_gates = (
        lax.all_gather(owned[0], REPLICA, axis=0, tiled=True),
        lax.all_gather(owned[1], REPLICA, axis=0, tiled=True),
        lax.all_gather(owned[2].astype(jnp.bfloat16), REPLICA, axis=0, tiled=True).astype(
            jnp.float32
        ),
    )
    gathered = column_inputs.reshape(-1, model_width)
    gate_pre = lax.dot_general(gathered, gate_weight, contract, preferred_element_type=jnp.float32)
    up_pre = lax.dot_general(gathered, up_weight, contract, preferred_element_type=jnp.float32)
    sigmoid_gate = jax.nn.sigmoid(gate_pre)
    active = gate_pre * sigmoid_gate
    hidden = (active * up_pre).astype(jnp.bfloat16)
    gathered_grad = column_grads.reshape(-1, model_width)
    row_gates = column_gates.reshape(-1)
    full_out = jnp.dot(hidden, down_weight, preferred_element_type=jnp.float32)
    partial_value = jnp.sum(gathered_grad * full_out, axis=1)
    summed_products = sum_at_owner(partial_value, REPLICA, 0)
    returned = lax.all_to_all(
        summed_products.reshape(owners, capacity), "expert", split_axis=0, concat_axis=0, tiled=True
    )
    gate_grad = jnp.sum(token_hot * returned.reshape(-1)[None, None, :], axis=2)
    scaled = (row_gates[:, None] * gathered_grad).astype(jnp.bfloat16)
    hidden_grad = lax.dot_general(scaled, down_weight, contract, preferred_element_type=jnp.float32)
    gate_pre_grad = (
        hidden_grad * up_pre * sigmoid_gate * (1.0 + gate_pre * (1.0 - sigmoid_gate))
    ).astype(jnp.bfloat16)
    up_pre_grad = (hidden_grad * active).astype(jnp.bfloat16)
    grad_down = lax.dot_general(hidden, scaled, leading, preferred_element_type=jnp.float32).astype(
        jnp.bfloat16
    )
    grad_gate = lax.dot_general(
        gate_pre_grad, gathered, leading, preferred_element_type=jnp.float32
    ).astype(jnp.bfloat16)
    grad_up = lax.dot_general(
        up_pre_grad, gathered, leading, preferred_element_type=jnp.float32
    ).astype(jnp.bfloat16)
    slot_grad = own_rows(
        jnp.dot(gate_pre_grad, gate_weight, preferred_element_type=jnp.float32)
        + jnp.dot(up_pre_grad, up_weight, preferred_element_type=jnp.float32),
        REPLICA,
    ).astype(jnp.bfloat16)
    slot_back = lax.all_to_all(
        slot_grad.reshape(owners, capacity, model_width),
        "expert",
        split_axis=0,
        concat_axis=0,
        tiled=True,
    )
    slot_back = slot_back.reshape(slot_count, model_width)
    input_grad = jnp.dot(dispatch, slot_back, preferred_element_type=jnp.float32).astype(
        jnp.bfloat16
    )
    return (gate_grad, input_grad, grad_gate[None], grad_up[None], grad_down[None])


def solution(mesh):
    torus = Mesh(
        mesh.devices.reshape(mesh.shape["expert"], 4, 8), ("expert", "replica_0", "replica_1")
    )
    in_specs = (
        P(EXPERT_REPLICA, None),
        P(EXPERT_REPLICA, None),
        P(EXPERT_REPLICA, None),
        P(EXPERT_REPLICA, None),
        P("expert", REPLICA, None),
        P("expert", REPLICA, None),
        P("expert", REPLICA, None),
    )
    out_specs = (
        P(EXPERT_REPLICA, None),
        P(EXPERT_REPLICA, None),
        P("expert", REPLICA, None),
        P("expert", REPLICA, None),
        P("expert", REPLICA, None),
    )
    return jax.shard_map(
        on_device, mesh=torus, in_specs=in_specs, out_specs=out_specs, check_vma=False
    )
```

profile of v0, /device:TPU:1, one launch (start us, length us, event | category | flops | bytes accessed | tf_op | source)
XLA Modules:
  0.0 404.9 jit_solution(4118786558378128443)
XLA Ops:
  7.2 0.9 copy.30
  8.1 0.1 eq.29
  8.2 0.2 convert_reduce_fusion
  8.5 0.1 convert_reduce_fusion.1
  8.6 1.1 convolution_convert_fusion.3
  9.6 0.1 reshape.81
  9.8 11.5 %all_to_all.42 = bf16[8,2,4096]{2,1,0:T(2,128)(2,1)} all-to-all(bf16[8,2,4096]{2,1,0:T(2,128)(2,1)S(1)} %reshape.81), channel_id=1, replica_groups=mesh['expert'=8,'replica_0'=4,'replica_1'=8] {'expert'}, dimensions={0} | all-to-all | bytes 262144 | tf_op jit(solution)/shard_map/all_to_all | solution.py:65
  21.3 1.1 convolution_convert_fusion.4
  22.4 0.1 reshape.80
  22.5 9.2 %all_to_all.43 = bf16[8,2,4096]{2,1,0:T(2,128)(2,1)} all-to-all(bf16[8,2,4096]{2,1,0:T(2,128)(2,1)S(1)} %reshape.80), channel_id=1, replica_groups=mesh['expert'=8,'replica_0'=4,'replica_1'=8] {'expert'}, dimensions={0} | all-to-all | bytes 262144 | tf_op jit(solution)/shard_map/all_to_all | solution.py:66
  31.7 68.7 %all-gather.6.cloned.1.call-done = bf16[256,2,4096]{2,1,0:T(2,128)(2,1)} async-done(((bf16[8,2,4096]{2,1,0:T(2,128)(2,1)}), bf16[256,2,4096]{2,1,0:T(2,128)(2,1)}) %all-gather.6.cloned.1.call-update) | async-done | bytes 4194320 | tf_op jit(solution)/shard_map/all_gather | solution.py:72
  100.4 7.2 %reshape.82 = bf16[512,4096]{1,0:T(8,128)(2,1)} reshape(bf16[256,2,4096]{2,1,0:T(2,128)(2,1)} %all-gather.6.cloned.1.call-done) | data formatting | bytes 8388608 | tf_op jit(solution)/shard_map/reshape | solution.py:78
  107.6 4.3 %fusion.12 = f32[512,224]{0,1:T(8,128)S(1)} fusion(bf16[512,4096]{1,0:T(8,128)(2,1)} %reshape.82, bf16[1,224,4096]{2,1,0:T(8,128)(2,1)} %param.11), kind=kOutput, calls=%fused_computation.22 | convolution fusion | flops 939524096 | bytes 6488064 | tf_op jit(solution)/shard_map/dot_general | solution.py:79
  112.0 2.3 multiply_convert_fusion.5
  114.3 67.3 %all-gather.4.cloned.1.call-done = bf16[256,2,4096]{2,1,0:T(2,128)(2,1)} async-done(((bf16[8,2,4096]{2,1,0:T(2,128)(2,1)}), bf16[256,2,4096]{2,1,0:T(2,128)(2,1)}) %all-gather.4.cloned.1.call-update) | async-done | bytes 4194320 | tf_op jit(solution)/shard_map/all_gather | solution.py:73
  181.6 7.6 %reshape.85 = f32[512,4096]{1,0:T(8,128)} reshape(bf16[256,2,4096]{2,1,0:T(2,128)(2,1)} %all-gather.4.cloned.1.call-done) | data formatting | bytes 12582912 | tf_op jit(solution)/shard_map/convert_element_type | solution.py:87
  189.2 5.3 %multiply_reduce_fusion = f32[512]{0:T(512)S(1)} fusion(f32[512,4096]{1,0:T(8,128)} %reshape.85, bf16[512,224]{0,1:T(8,128)(2,1)S(1)} %get-tuple-element.14, bf16[1,224,4096]{2,1,0:T(8,128)(2,1)} %param.13), kind=kOutput, calls=%fused_computation.3 | convolution fusion | flops 943717888 | bytes 10455040 | tf_op jit(solution)/shard_map/dot_general | solution.py:86
  194.5 0.1 all_to_all.29
  194.6 14.5 %all_to_all.44 = f32[32,1,16]{2,1,0:T(1,128)S(1)} all-to-all(f32[32,1,16]{2,1,0:T(1,128)S(1)} %bitcast.46), channel_id=1, replica_groups=mesh['expert'=8,'replica_0'=4,'replica_1'=8] {'replica_0','replica_1'}, dimensions={0} | all-to-all | bytes 4096 | tf_op jit(solution)/shard_map/all_to_all | solution.py:19
  209.1 0.7 all_to_all.31
  209.8 8.9 %all-to-all-start.3 = ((f32[8,1,2]{2,1,0:T(1,128)}), f32[8,1,2]{2,1,0:T(1,128)S(1)}, u32[]{:S(2)}, u32[]{:S(2)}) async-start(f32[8,1,2]{2,1,0:T(1,128)} %bitcast.4), calls=%async_computation.3 | async-start | bytes 8192 | tf_op jit(solution)/shard_map/all_to_all | solution.py:89
  218.7 0.1 copy.34
  218.8 4.4 %all-to-all-done.3 = f32[8,1,2]{2,1,0:T(1,128)S(1)} async-done(((f32[8,1,2]{2,1,0:T(1,128)}), f32[8,1,2]{2,1,0:T(1,128)S(1)}, u32[]{:S(2)}, u32[]{:S(2)}) %all-to-all-start.3) | async-done | bytes 96 | tf_op jit(solution)/shard_map/all_to_all | solution.py:89
  223.3 0.5 broadcast.41
  223.8 0.7 reduce.8
  224.5 0.2 select_reduce_fusion
  224.7 0.1 convert_element_type.102
  224.8 7.6 %all_to_all.45 = bf16[8,1,2]{2,1,0:T(2,128)(2,1)S(1)} all-to-all(bf16[8,1,2]{2,1,0:T(2,128)(2,1)S(1)} %convert_element_type.102), channel_id=1, replica_groups=mesh['expert'=8,'replica_0'=4,'replica_1'=8] {'expert'}, dimensions={0} | all-to-all | bytes 64 | tf_op jit(solution)/shard_map/all_to_all | solution.py:67
  232.4 31.3 %all-gather = bf16[256,1,2]{2,1,0:T(2,128)(2,1)S(1)} all-gather(bf16[8,1,2]{2,1,0:T(2,128)(2,1)S(1)} %all_to_all.45), channel_id=2, replica_groups=mesh['expert'=8,'replica_0'=4,'replica_1'=8] {'replica_0','replica_1'}, dimensions={0}, use_global_device_ids=true | all-gather | bytes 1056 | tf_op jit(solution)/shard_map/all_gather | solution.py:74
  263.7 0.1 convert_element_type.101
  263.8 10.4 %multiply_convert_fusion.1 = bf16[256,2,4096]{2,1,0:T(2,128)(2,1)} fusion(f32[256,2]{1,0:T(8,128)S(1)} %bitcast.45, bf16[256,2,4096]{2,1,0:T(2,128)(2,1)} %all-gather.4.cloned.1.call-done), kind=kLoop, calls=%fused_computation.2 | loop fusion | flops 6291456 | bytes 8390656 | tf_op jit(solution)/shard_map/convert_element_type | solution.py:93
  274.2 7.2 %convert_element_type.91 = bf16[512,4096]{1,0:T(8,128)(2,1)} reshape(bf16[256,2,4096]{2,1,0:T(2,128)(2,1)} %multiply_convert_fusion.1) | data formatting | bytes 8388608 | tf_op jit(solution)/shard_map/convert_element_type | solution.py:93
  281.4 4.4 %multiply_convert_fusion.3 = (bf16[512,224]{0,1:T(8,128)(2,1)S(1)}, bf16[512,224]{0,1:T(8,128)(2,1)S(1)}) fusion(f32[512,224]{0,1:T(8,128)S(1)} %fusion.12, f32[512,224]{0,1:T(8,128)} %get-tuple-element.15, bf16[512,4096]{1,0:T(8,128)(2,1)} %convert_element_type.91, bf16[1,224,4096]{2,1,0:T(8,128)(2,1)} %param.13), kind=kOutput, calls=%fused_computation.24 | convolution fusion | flops 941015040 | bytes 7405568 | tf_op jit(solution)/shard_map/dot_general | solution.py:94
  285.8 1.3 fusion.10
  287.1 3.3 add_convert_fusion
  290.5 0.3 reduce-scatter.5.cloned.1.call-start
  290.7 53.7 %reduce-scatter.3.cloned.1.call-done = bf16[128,4096]{1,0:T(8,128)(2,1)} async-done(((bf16[512,4096]{1,0:T(8,128)(2,1)}), bf16[128,4096]{1,0:T(8,128)(2,1)}) %reduce-scatter.3.cloned.1.call-update) | async-done | bytes 1048592 | tf_op jit(solution)/shard_map/reduce_scatter | solution.py:26
  344.5 0.6 copy.36
  345.1 0.4 convert_reduce_fusion.2
  345.5 0.1 mul.80
  345.6 4.5 %fusion.1 = bf16[1,224,4096]{2,1,0:T(8,128)(2,1)} fusion(bf16[512,224]{0,1:T(8,128)(2,1)S(1)} %get-tuple-element.12, bf16[512,4096]{1,0:T(8,128)(2,1)} %reshape.82), kind=kOutput, calls=%fused_computation.8 | convolution fusion | flops 940441600 | bytes 6258688 | tf_op jit(solution)/shard_map/dot_general | solution.py:105
  350.2 5.8 %fusion.2 = bf16[1,224,4096]{2,1,0:T(8,128)(2,1)} fusion(bf16[512,224]{0,1:T(8,128)(2,1)S(1)} %get-tuple-element.14, f32[512,4096]{1,0:T(8,128)} %reshape.85, f32[512]{0:T(512)S(1)} %mul.80), kind=kOutput, calls=%fused_computation.9 | convolution fusion | flops 944635904 | bytes 10455040 | tf_op jit(solution)/shard_map/dot_general | solution.py:99
  356.0 24.6 %reduce-scatter.5.cloned.1.call-done = bf16[16,4096]{1,0:T(8,128)(2,1)} async-done(((bf16[128,4096]{1,0:T(8,128)(2,1)}), bf16[16,4096]{1,0:T(8,128)(2,1)}) %reduce-scatter.5.cloned.1.call-update) | async-done | bytes 131088 | tf_op jit(solution)/shard_map/reduce_scatter | solution.py:26
  380.6 1.6 reshape.83
  382.3 10.0 %all-to-all-start.5 = ((bf16[8,2,4096]{2,1,0:T(2,128)(2,1)}), bf16[8,2,4096]{2,1,0:T(2,128)(2,1)S(1)}, u32[]{:S(2)}, u32[]{:S(2)}) async-start(bf16[8,2,4096]{2,1,0:T(2,128)(2,1)} %reshape.83), calls=%async_computation.7 | async-start | bytes 262144 | tf_op jit(solution)/shard_map/all_to_all | solution.py:113
  392.3 4.5 %fusion = bf16[1,224,4096]{2,1,0:T(8,128)(2,1)} fusion(bf16[512,224]{0,1:T(8,128)(2,1)S(1)} %get-tuple-element.13, bf16[512,4096]{1,0:T(8,128)(2,1)} %reshape.82), kind=kOutput, calls=%fused_computation.7 | convolution fusion | flops 940441600 | bytes 6258688 | tf_op jit(solution)/shard_map/dot_general | solution.py:102
  396.8 0.7 all-to-all-done.5
  397.6 0.8 convolution_convert_fusion.5
  (20 shorter events, 0.4 us)
Async XLA Ops:
  7.2 104.8 %copy-start = (bf16[1,224,4096]{2,1,0:T(8,128)(2,1)S(1)}, bf16[1,224,4096]{2,1,0:T(8,128)(2,1)}, u32[]{:S(2)}) copy-start(bf16[1,224,4096]{2,1,0:T(8,128)(2,1)} %param.12) | copy-start | bytes 5505028
  7.2 93.2 %all-gather.6.cloned.1.call-start = ((), (), s32[]{:S(2)}) async-start(), calls=%async_computation.9 | async-start | bytes 4325376 | tf_op jit(solution)/shard_map/all_gather | solution.py:72
  21.3 160.3 %all-gather.4.cloned.1.call-start = ((), (), s32[]{:S(2)}) async-start(), calls=%async_computation.8 | async-start | bytes 4325376 | tf_op jit(solution)/shard_map/all_gather | solution.py:73
  107.6 4.4 %copy-start.1 = (bf16[512,4096]{1,0:T(8,128)(2,1)S(1)}, bf16[512,4096]{1,0:T(8,128)(2,1)}, u32[]{:S(2)}) copy-start(bf16[512,4096]{1,0:T(8,128)(2,1)} %reshape.82) | copy-start | bytes 12582916
  189.2 29.6 %copy-start.3 = (f32[6,2]{0,1:T(2,128)S(1)}, f32[6,2]{0,1:T(2,128)}, u32[]{:S(2)}) copy-start(f32[6,2]{0,1:T(2,128)} %param.10) | copy-start | bytes 148
  209.8 13.5 %all-to-all-start.3 = ((f32[8,1,2]{2,1,0:T(1,128)}), f32[8,1,2]{2,1,0:T(1,128)S(1)}, u32[]{:S(2)}, u32[]{:S(2)}) async-start(f32[8,1,2]{2,1,0:T(1,128)} %bitcast.4), calls=%async_computation.3 | async-start | bytes 8192 | tf_op jit(solution)/shard_map/all_to_all | solution.py:89
  218.7 125.7 %reduce-scatter.3.cloned.1.call-start = ((), (), s32[]{:S(2)}) async-start(), calls=%async_computation.10 | async-start | bytes 5242880 | tf_op jit(solution)/shard_map/reduce_scatter | solution.py:26
  281.4 4.4 %copy-start.2 = (bf16[1,224,4096]{2,1,0:T(8,128)(2,1)S(1)}, bf16[1,224,4096]{2,1,0:T(8,128)(2,1)}, u32[]{:S(2)}) copy-start(bf16[1,224,4096]{2,1,0:T(8,128)(2,1)} %param.11) | copy-start | bytes 5505028
  290.5 90.2 %reduce-scatter.5.cloned.1.call-start = ((), (), s32[]{:S(2)}) async-start(), calls=%async_computation.11 | async-start | bytes 1179648 | tf_op jit(solution)/shard_map/reduce_scatter | solution.py:26
  382.3 15.3 %all-to-all-start.5 = ((bf16[8,2,4096]{2,1,0:T(2,128)(2,1)}), bf16[8,2,4096]{2,1,0:T(2,128)(2,1)S(1)}, u32[]{:S(2)}, u32[]{:S(2)}) async-start(bf16[8,2,4096]{2,1,0:T(2,128)(2,1)} %reshape.83), calls=%async_computation.7 | async-start | bytes 262144 | tf_op jit(solution)/shard_map/all_to_all | solution.py:113
Sparse Core Ops, SparseCore 0:
  21.4 78.9 all-gather.5
  103.0 78.5 all-gather.3
  290.6 53.7 reduce-scatter.2
  346.8 33.7 reduce-scatter.4
where the time goes:
time: 406 us; the launch traced here: 405 us
  waiting for transfers between devices  220 us (54%)
  blocking collectives  74 us (18%)
  matrix products  38.8 us (10%)
  local copies, waits for them, and re-layouts  27.3 us (7%)
  starting transfers between devices  19.3 us (5%)
  between operations  13.9 us (3%)
  other arithmetic  12.1 us (3%)
    reduce_scatter x2, waiting for transfers between devices, own_rows(): running = lax.psum_scatter(running, axis, scatter_dimension=0, tiled=True)  78.3 us
    all_gather x1, waiting for transfers between devices, on_device(): lax.all_gather(owned[0], REPLICA, axis=0, tiled=True)  68.7 us
    all_gather x1, waiting for transfers between devices, on_device(): lax.all_gather(owned[1], REPLICA, axis=0, tiled=True)  67.3 us
    all_gather x1, blocking collectives, on_device(): lax.all_gather(owned[2].astype(jnp.bfloat16), REPLICA, axis=0, tiled=True)  31.3 us
    all_to_all x1, blocking collectives, sum_at_owner(): tiles = lax.all_to_all(split_up(value, dim, peers), axis, 0, 0, tiled=True)  14.5 us
    all_to_all x1, blocking collectives, on_device(): lax.all_to_all(send_inputs, 'expert', split_axis=0, concat_axis=0, tiled=...  11.5 us
    convert_element_type x1, other arithmetic, on_device(): scaled = (row_gates[:, None] * gathered_grad).astype(jnp.bfloat16)  10.4 us
    all_to_all x1, starting transfers between devices, on_device(): lax.all_to_all(slot_grad.reshape(owners, capacity, model_width), 'expert'...  10 us
  transfers between devices with their start and end apart: 6, of which 6 were waited for; matrix products, arithmetic and copies ran while one was open for 8% of the time, Pallas kernels for 0%

commit v1 on v0

--- a/solution.py
+++ b/solution.py
@@ -71,9 +71,12 @@
     column_inputs, column_grads, column_gates = (
         lax.all_gather(owned[0], REPLICA, axis=0, tiled=True),
         lax.all_gather(owned[1], REPLICA, axis=0, tiled=True),
-        lax.all_gather(owned[2].astype(jnp.bfloat16), REPLICA, axis=0, tiled=True).astype(
-            jnp.float32
-        ),
+        jnp.concatenate(
+            lax.all_to_all(
+                jnp.stack([owned[2].astype(jnp.bfloat16)] * lax.axis_size(REPLICA)), REPLICA, 0, 0
+            ),
+            axis=0,
+        ).astype(jnp.float32),
     )
     gathered = column_inputs.reshape(-1, model_width)
     gate_pre = lax.dot_general(gathered, gate_weight, contract, preferred_element_type=jnp.float32)

time: 406 us -> 376 us (0.926)
  blocking collectives: 74 us -> 54.4 us
  waiting for transfers between devices: 220 us -> 210 us
    all_gather x1 -> x0, blocking collectives: 31.3 us -> none  [on_device(): lax.all_gather(owned[2].astype(jnp.bfloat16), REPLICA, axis=0, tiled=True)]
    all_to_all x0 -> x1, blocking collectives: none -> 11.6 us  [on_device(): lax.all_to_all(jnp.stack([owned[2].astype(jnp.bfloat16)] * lax.axis_size(...]
    reduce_scatter x2, waiting for transfers between devices: 78.3 us -> 68.8 us  [own_rows(): running = lax.psum_scatter(running, axis, scatter_dimension=0, tiled=True)]
where the time goes in v1:
time: 376 us; the launch traced here: 375 us
  waiting for transfers between devices  210 us (56%)
  blocking collectives  54.4 us (14%)
  matrix products  38.8 us (10%)
  local copies, waits for them, and re-layouts  27.6 us (7%)
  starting transfers between devices  18.6 us (5%)
  between operations  13.9 us (4%)
  other arithmetic  11.5 us (3%)
    reduce_scatter x2, waiting for transfers between devices, own_rows(): running = lax.psum_scatter(running, axis, scatter_dimension=0, tiled=True)  68.8 us
    all_gather x1, waiting for transfers between devices, on_device(): lax.all_gather(owned[0], REPLICA, axis=0, tiled=True)  68.7 us
    all_gather x1, waiting for transfers between devices, on_device(): lax.all_gather(owned[1], REPLICA, axis=0, tiled=True)  67.3 us
    all_to_all x1, blocking collectives, sum_at_owner(): tiles = lax.all_to_all(split_up(value, dim, peers), axis, 0, 0, tiled=True)  14.5 us
    all_to_all x1, blocking collectives, on_device(): lax.all_to_all(jnp.stack([owned[2].astype(jnp.bfloat16)] * lax.axis_size(...  11.6 us
    all_to_all x1, blocking collectives, on_device(): lax.all_to_all(send_inputs, 'expert', split_axis=0, concat_axis=0, tiled=...  11.5 us
    convert_element_type x1, other arithmetic, on_device(): scaled = (row_gates[:, None] * gathered_grad).astype(jnp.bfloat16)  10.4 us
    all_to_all x1, starting transfers between devices, on_device(): lax.all_to_all(slot_grad.reshape(owners, capacity, model_width), 'expert'...  9.54 us
  transfers between devices with their start and end apart: 6, of which 6 were waited for; matrix products, arithmetic and copies ran while one was open for 8% of the time, Pallas kernels for 0%

profile of v1, /device:TPU:1, one launch (start us, length us, event | category | flops | bytes accessed | tf_op | source)
XLA Modules:
  0.0 374.9 jit_solution(14969689032543285102)
XLA Ops:
  7.2 0.9 copy.51
  8.1 0.1 eq.29
  8.2 0.2 convert_reduce_fusion
  8.5 0.1 convert_reduce_fusion.1
  8.6 1.1 convolution_convert_fusion.3
  9.6 0.1 reshape.94
  9.8 11.5 %all_to_all.44 = bf16[8,2,4096]{2,1,0:T(2,128)(2,1)} all-to-all(bf16[8,2,4096]{2,1,0:T(2,128)(2,1)S(1)} %reshape.94), channel_id=1, replica_groups=mesh['expert'=8,'replica_0'=4,'replica_1'=8] {'expert'}, dimensions={0} | all-to-all | bytes 262144 | tf_op jit(solution)/shard_map/all_to_all | solution.py:65
  21.3 1.1 convolution_convert_fusion.4
  22.4 0.1 reshape.93
  22.5 9.2 %all_to_all.45 = bf16[8,2,4096]{2,1,0:T(2,128)(2,1)} all-to-all(bf16[8,2,4096]{2,1,0:T(2,128)(2,1)S(1)} %reshape.93), channel_id=1, replica_groups=mesh['expert'=8,'replica_0'=4,'replica_1'=8] {'expert'}, dimensions={0} | all-to-all | bytes 262144 | tf_op jit(solution)/shard_map/all_to_all | solution.py:66
  31.7 68.7 %all-gather.5.cloned.1.call-done = bf16[256,2,4096]{2,1,0:T(2,128)(2,1)} async-done(((bf16[8,2,4096]{2,1,0:T(2,128)(2,1)}), bf16[256,2,4096]{2,1,0:T(2,128)(2,1)}) %all-gather.5.cloned.1.call-update) | async-done | bytes 4194320 | tf_op jit(solution)/shard_map/all_gather | solution.py:72
  100.4 7.2 %reshape.95 = bf16[512,4096]{1,0:T(8,128)(2,1)} reshape(bf16[256,2,4096]{2,1,0:T(2,128)(2,1)} %all-gather.5.cloned.1.call-done) | data formatting | bytes 8388608 | tf_op jit(solution)/shard_map/reshape | solution.py:81
  107.6 4.3 %fusion.12 = f32[512,224]{0,1:T(8,128)S(1)} fusion(bf16[512,4096]{1,0:T(8,128)(2,1)} %reshape.95, bf16[1,224,4096]{2,1,0:T(8,128)(2,1)} %param.11), kind=kOutput, calls=%fused_computation.22 | convolution fusion | flops 939524096 | bytes 6488064 | tf_op jit(solution)/shard_map/dot_general | solution.py:82
  112.0 2.3 multiply_convert_fusion.5
  114.3 67.3 %all-gather.3.cloned.1.call-done = bf16[256,2,4096]{2,1,0:T(2,128)(2,1)} async-done(((bf16[8,2,4096]{2,1,0:T(2,128)(2,1)}), bf16[256,2,4096]{2,1,0:T(2,128)(2,1)}) %all-gather.3.cloned.1.call-update) | async-done | bytes 4194320 | tf_op jit(solution)/shard_map/all_gather | solution.py:73
  181.6 7.6 %reshape.98 = f32[512,4096]{1,0:T(8,128)} reshape(bf16[256,2,4096]{2,1,0:T(2,128)(2,1)} %all-gather.3.cloned.1.call-done) | data formatting | bytes 12582912 | tf_op jit(solution)/shard_map/convert_element_type | solution.py:90
  189.2 5.3 %multiply_reduce_fusion = f32[512]{0:T(512)S(1)} fusion(f32[512,4096]{1,0:T(8,128)} %reshape.98, bf16[512,224]{0,1:T(8,128)(2,1)S(1)} %get-tuple-element.19, bf16[1,224,4096]{2,1,0:T(8,128)(2,1)} %param.13), kind=kOutput, calls=%fused_computation.3 | convolution fusion | flops 943717888 | bytes 10455040 | tf_op jit(solution)/shard_map/dot_general | solution.py:89
  194.5 0.1 all_to_all.30
  194.6 14.5 %all_to_all.46 = f32[32,1,16]{2,1,0:T(1,128)S(1)} all-to-all(f32[32,1,16]{2,1,0:T(1,128)S(1)} %bitcast.47), channel_id=1, replica_groups=mesh['expert'=8,'replica_0'=4,'replica_1'=8] {'replica_0','replica_1'}, dimensions={0} | all-to-all | bytes 4096 | tf_op jit(solution)/shard_map/all_to_all | solution.py:19
  209.1 0.7 all_to_all.32
  209.8 8.9 %all-to-all-start.3 = ((f32[8,1,2]{2,1,0:T(1,128)}), f32[8,1,2]{2,1,0:T(1,128)S(1)}, u32[]{:S(2)}, u32[]{:S(2)}) async-start(f32[8,1,2]{2,1,0:T(1,128)} %bitcast.4), calls=%async_computation.3 | async-start | bytes 8192 | tf_op jit(solution)/shard_map/all_to_all | solution.py:92
  218.7 0.1 copy.55
  218.8 4.4 %all-to-all-done.3 = f32[8,1,2]{2,1,0:T(1,128)S(1)} async-done(((f32[8,1,2]{2,1,0:T(1,128)}), f32[8,1,2]{2,1,0:T(1,128)S(1)}, u32[]{:S(2)}, u32[]{:S(2)}) %all-to-all-start.3) | async-done | bytes 96 | tf_op jit(solution)/shard_map/all_to_all | solution.py:92
  223.3 0.5 broadcast.38
  223.8 0.7 reduce.4
  224.5 0.2 select_reduce_fusion
  224.7 0.1 convert_element_type.119
  224.8 7.6 %all_to_all.47 = bf16[8,1,2]{2,1,0:T(2,128)(2,1)S(1)} all-to-all(bf16[8,1,2]{2,1,0:T(2,128)(2,1)S(1)} %convert_element_type.119), channel_id=1, replica_groups=mesh['expert'=8,'replica_0'=4,'replica_1'=8] {'expert'}, dimensions={0} | all-to-all | bytes 64 | tf_op jit(solution)/shard_map/all_to_all | solution.py:67
  232.4 0.1 copy.57
  232.5 11.6 %all_to_all.48 = bf16[32,8,2]{1,2,0:T(2,128)(2,1)S(1)} all-to-all(bf16[32,8,2]{1,2,0:T(2,128)(2,1)S(1)} %stack.5), channel_id=1, replica_groups=mesh['expert'=8,'replica_0'=4,'replica_1'=8] {'replica_0','replica_1'}, dimensions={0} | all-to-all | bytes 2048 | tf_op jit(solution)/shard_map/all_to_all | solution.py:75
  244.1 0.1 copy.58
  244.2 0.2 copy.63
  244.4 10.4 %multiply_convert_fusion.1 = bf16[256,2,4096]{2,1,0:T(2,128)(2,1)} fusion(f32[256,2]{1,0:T(8,128)S(1)} %bitcast.46, bf16[256,2,4096]{2,1,0:T(2,128)(2,1)} %all-gather.3.cloned.1.call-done), kind=kLoop, calls=%fused_computation.2 | loop fusion | flops 6291456 | bytes 8390656 | tf_op jit(solution)/shard_map/convert_element_type | solution.py:96
  254.8 7.2 %convert_element_type.105 = bf16[512,4096]{1,0:T(8,128)(2,1)} reshape(bf16[256,2,4096]{2,1,0:T(2,128)(2,1)} %multiply_convert_fusion.1) | data formatting | bytes 8388608 | tf_op jit(solution)/shard_map/convert_element_type | solution.py:96
  262.0 4.4 %multiply_convert_fusion.3 = (bf16[512,224]{0,1:T(8,128)(2,1)S(1)}, bf16[512,224]{0,1:T(8,128)(2,1)S(1)}) fusion(f32[512,224]{0,1:T(8,128)S(1)} %fusion.12, f32[512,224]{0,1:T(8,128)} %get-tuple-element.20, bf16[512,4096]{1,0:T(8,128)(2,1)} %convert_element_type.105, bf16[1,224,4096]{2,1,0:T(8,128)(2,1)} %param.13), kind=kOutput, calls=%fused_computation.24 | convolution fusion | flops 941015040 | bytes 7405568 | tf_op jit(solution)/shard_map/dot_general | solution.py:97
  266.4 1.3 fusion.10
  267.7 3.3 add_convert_fusion
  271.1 43.2 %reduce-scatter.3.cloned.1.call-done = bf16[128,4096]{1,0:T(8,128)(2,1)} async-done(((bf16[512,4096]{1,0:T(8,128)(2,1)}), bf16[128,4096]{1,0:T(8,128)(2,1)}) %reduce-scatter.3.cloned.1.call-update) | async-done | bytes 1048592 | tf_op jit(solution)/shard_map/reduce_scatter | solution.py:26
  314.4 0.6 copy.62
  315.0 0.1 reshape.100
  315.2 4.5 %fusion.1 = bf16[1,224,4096]{2,1,0:T(8,128)(2,1)} fusion(bf16[512,224]{0,1:T(8,128)(2,1)S(1)} %get-tuple-element.17, bf16[512,4096]{1,0:T(8,128)(2,1)} %reshape.95), kind=kOutput, calls=%fused_computation.8 | convolution fusion | flops 940441600 | bytes 6258688 | tf_op jit(solution)/shard_map/dot_general | solution.py:108
  319.7 5.8 %fusion.2 = bf16[1,224,4096]{2,1,0:T(8,128)(2,1)} fusion(bf16[512,224]{0,1:T(8,128)(2,1)S(1)} %get-tuple-element.19, f32[512,4096]{1,0:T(8,128)} %reshape.98, f32[512]{0:T(512)S(1)} %reshape.100), kind=kOutput, calls=%fused_computation.9 | convolution fusion | flops 944635904 | bytes 10455040 | tf_op jit(solution)/shard_map/dot_general | solution.py:102
  325.5 25.5 %reduce-scatter.5.cloned.1.call-done = bf16[16,4096]{1,0:T(8,128)(2,1)} async-done(((bf16[128,4096]{1,0:T(8,128)(2,1)}), bf16[16,4096]{1,0:T(8,128)(2,1)}) %reduce-scatter.5.cloned.1.call-update) | async-done | bytes 131088 | tf_op jit(solution)/shard_map/reduce_scatter | solution.py:26
  351.1 1.6 reshape.96
  352.7 9.5 %all-to-all-start.6 = ((bf16[8,2,4096]{2,1,0:T(2,128)(2,1)}), bf16[8,2,4096]{2,1,0:T(2,128)(2,1)S(1)}, u32[]{:S(2)}, u32[]{:S(2)}) async-start(bf16[8,2,4096]{2,1,0:T(2,128)(2,1)} %reshape.96), calls=%async_computation.8 | async-start | bytes 262144 | tf_op jit(solution)/shard_map/all_to_all | solution.py:116
  362.2 4.5 %fusion = bf16[1,224,4096]{2,1,0:T(8,128)(2,1)} fusion(bf16[512,224]{0,1:T(8,128)(2,1)S(1)} %get-tuple-element.18, bf16[512,4096]{1,0:T(8,128)(2,1)} %reshape.95), kind=kOutput, calls=%fused_computation.7 | convolution fusion | flops 940441600 | bytes 6258688 | tf_op jit(solution)/shard_map/dot_general | solution.py:105
  366.8 0.7 all-to-all-done.6
  367.5 0.8 convolution_convert_fusion.5
  (22 shorter events, 0.5 us)
Async XLA Ops:
  7.2 104.8 %copy-start = (bf16[1,224,4096]{2,1,0:T(8,128)(2,1)S(1)}, bf16[1,224,4096]{2,1,0:T(8,128)(2,1)}, u32[]{:S(2)}) copy-start(bf16[1,224,4096]{2,1,0:T(8,128)(2,1)} %param.12) | copy-start | bytes 5505028
  7.2 93.2 %all-gather.5.cloned.1.call-start = ((), (), s32[]{:S(2)}) async-start(), calls=%async_computation.10 | async-start | bytes 4325376 | tf_op jit(solution)/shard_map/all_gather | solution.py:72
  21.3 160.3 %all-gather.3.cloned.1.call-start = ((), (), s32[]{:S(2)}) async-start(), calls=%async_computation.9 | async-start | bytes 4325376 | tf_op jit(solution)/shard_map/all_gather | solution.py:73
  107.6 4.4 %copy-start.1 = (bf16[512,4096]{1,0:T(8,128)(2,1)S(1)}, bf16[512,4096]{1,0:T(8,128)(2,1)}, u32[]{:S(2)}) copy-start(bf16[512,4096]{1,0:T(8,128)(2,1)} %reshape.95) | copy-start | bytes 12582916
  189.2 29.6 %copy-start.3 = (f32[6,2]{0,1:T(2,128)S(1)}, f32[6,2]{0,1:T(2,128)}, u32[]{:S(2)}) copy-start(f32[6,2]{0,1:T(2,128)} %param.10) | copy-start | bytes 148
  209.8 13.5 %all-to-all-start.3 = ((f32[8,1,2]{2,1,0:T(1,128)}), f32[8,1,2]{2,1,0:T(1,128)S(1)}, u32[]{:S(2)}, u32[]{:S(2)}) async-start(f32[8,1,2]{2,1,0:T(1,128)} %bitcast.4), calls=%async_computation.3 | async-start | bytes 8192 | tf_op jit(solution)/shard_map/all_to_all | solution.py:92
  218.7 95.6 %reduce-scatter.3.cloned.1.call-start = ((), (), s32[]{:S(2)}) async-start(), calls=%async_computation.11 | async-start | bytes 5242880 | tf_op jit(solution)/shard_map/reduce_scatter | solution.py:26
  262.0 4.5 %copy-start.2 = (bf16[1,224,4096]{2,1,0:T(8,128)(2,1)S(1)}, bf16[1,224,4096]{2,1,0:T(8,128)(2,1)}, u32[]{:S(2)}) copy-start(bf16[1,224,4096]{2,1,0:T(8,128)(2,1)} %param.11) | copy-start | bytes 5505028
  271.1 80.0 %reduce-scatter.5.cloned.1.call-start = ((), (), s32[]{:S(2)}) async-start(), calls=%async_computation.12 | async-start | bytes 1179648 | tf_op jit(solution)/shard_map/reduce_scatter | solution.py:26
  352.7 14.8 %all-to-all-start.6 = ((bf16[8,2,4096]{2,1,0:T(2,128)(2,1)}), bf16[8,2,4096]{2,1,0:T(2,128)(2,1)S(1)}, u32[]{:S(2)}, u32[]{:S(2)}) async-start(bf16[8,2,4096]{2,1,0:T(2,128)(2,1)} %reshape.96), calls=%async_computation.8 | async-start | bytes 262144 | tf_op jit(solution)/shard_map/all_to_all | solution.py:116
Sparse Core Ops, SparseCore 0:
  21.4 78.9 all-gather.4
  103.0 78.5 all-gather.2
  271.2 43.1 reduce-scatter.2
  316.8 34.2 reduce-scatter.4
